TPU v7x, 32 devices: a whole 2x2x4 slice. The times are simulated.
32 devices in a mesh: grp: 2 (over y), tx: 4 (over z), ty: 4 (over x, core).
Axes of the slice: x: 2, y: 2, z: 4, core: 2. Of those that a mesh axis runs over, the one named last changes fastest.
Arguments:
- obj_field: float32 [2, 1024, 512], P(None, ('grp', 'tx'), 'ty'), parts along dimension 1, may hold values from -6 to 6
- eigenprobes: bfloat16 [2, 32, 128, 128], P(None, 'grp'), parts along dimension 1, may hold values from -1.5 to 1.5
- weights: float32 [8, 4, 3, 16], P(('grp', 'tx'), 'ty'), parts along dimension 0, may hold values from -4 to 4
- offsets: int32 [8, 4, 3, 2], P(('grp', 'tx'), 'ty'), parts along dimension 0, may hold values from 0 to 127
- counts: int32 [8, 4], P(('grp', 'tx'), 'ty'), parts along dimension 0, may hold values from 1 to 3, as said below
- amplitudes: bfloat16 [8, 4, 3, 128, 128], P(('grp', 'tx'), 'ty'), parts along dimension 0, may hold values from 0.19921875 to 3
Outputs:
- new_object: float32 [2, 1024, 512], P(None, ('grp', 'tx'), 'ty'), parts along dimension 1
- new_eigenprobes: float32 [2, 32, 128, 128], P(None, 'grp'), parts along dimension 1
There are 2 independent parts, one for each index of `grp`. A program takes and returns all parts, laid end to end along the dimension named above; each array names one. Nothing has to cross between parts.
Inputs may be any that keep to these rules, and one draw needn't show every extreme that they name: Every tile holds 1 to 3 positions; some tile holds exactly 3; slots from counts on are unused.
All inputs are finite; a program needn't handle non-finite values.
Results may differ from a plain program's by a relative error of at most 0.0003.
Values sent between devices are 32-bit elements; how exact they have to be, the bound alone decides.
A program may use at most 64 MiB of HBM per device.

v0:
```python
import math

import jax
import jax.numpy as jnp
from jax import lax
from jax.sharding import PartitionSpec as P

high = lax.Precision.HIGHEST


def from_behind(value, axis, steps):
    count = lax.axis_size(axis)
    pairs = [(source, (source + steps) % count) for source in range(count)]
    return lax.ppermute(value, axis, pairs)


def tables(frame, sign):
    grid = jnp.arange(frame, dtype=jnp.int32)
    phase = grid[:, None] * grid[None, :] % frame
    angle = phase.astype(jnp.float32) * (2.0 * math.pi / frame)
    scale = 1.0 / math.sqrt(frame)
    return (jnp.cos(angle) * scale, sign * jnp.sin(angle) * scale)


def transform(real_part, imag_part, table_re, table_im):
    left_re = jnp.einsum("jk,skl->sjl", table_re, real_part, precision=high) - jnp.einsum(
        "jk,skl->sjl", table_im, imag_part, precision=high
    )
    left_im = jnp.einsum("jk,skl->sjl", table_re, imag_part, precision=high) + jnp.einsum(
        "jk,skl->sjl", table_im, real_part, precision=high
    )
    out_re = jnp.einsum("sjk,kl->sjl", left_re, table_re, precision=high) - jnp.einsum(
        "sjk,kl->sjl", left_im, table_im, precision=high
    )
    out_im = jnp.einsum("sjk,kl->sjl", left_re, table_im, precision=high) + jnp.einsum(
        "sjk,kl->sjl", left_im, table_re, precision=high
    )
    return (out_re, out_im)


def row_divisor(norms, start, count, frame, modes):
    mode_of_row = (start + jnp.arange(count, dtype=jnp.int32)) // frame % modes
    match = mode_of_row[:, None] == jnp.arange(modes, dtype=jnp.int32)[None, :]
    return jnp.sum(jnp.where(match, norms[None, :] + 1.0, 0.0), axis=1)


def per_device(obj_field, eigenprobes, weights, offsets, counts, amplitudes):
    tile = obj_field.shape[1]
    modes = eigenprobes.shape[1]
    frame = eigenprobes.shape[2]
    slots = weights.shape[2]
    wts = weights[0, 0]
    offs = offsets[0, 0]
    live = (jnp.arange(slots, dtype=jnp.int32) < counts[0, 0]).astype(jnp.float32)
    local_norms = jnp.sum(live[:, None] * wts * wts, axis=0)
    below = from_behind(obj_field, "tx", -1)
    tall = jnp.concatenate([obj_field, below], axis=1)
    beside = from_behind(tall, "ty", -1)
    region = jnp.concatenate([tall, beside], axis=2)
    zero_index = jnp.int32(0)

    def read_window(row_start, col_start):
        return lax.dynamic_slice(region, (zero_index, row_start, col_start), (2, frame, frame))

    windows = jax.vmap(read_window)(offs[:, 0], offs[:, 1])
    win_re = windows[:, 0]
    win_im = windows[:, 1]
    eig32 = eigenprobes.astype(jnp.float32)
    probe = jnp.einsum("sk,ckij->csij", wts, eig32, precision=high)
    psi_re = probe[0] * win_re - probe[1] * win_im
    psi_im = probe[0] * win_im + probe[1] * win_re
    fwd_re, fwd_im = tables(frame, -1.0)
    spec_re, spec_im = transform(psi_re, psi_im, fwd_re, fwd_im)
    amps = amplitudes[0, 0].astype(jnp.float32)
    factor = (amps / jnp.sqrt(spec_re * spec_re + spec_im * spec_im + 0.25) - 1.0) * live[
        :, None, None
    ]
    inv_re, inv_im = tables(frame, 1.0)
    chi_re, chi_im = transform(spec_re * factor, spec_im * factor, inv_re, inv_im)
    obj_re = probe[0] * chi_re + probe[1] * chi_im
    obj_im = probe[0] * chi_im - probe[1] * chi_re
    power = (probe[0] * probe[0] + probe[1] * probe[1]) * live[:, None, None]
    pieces = jnp.stack([obj_re, obj_im, power], axis=1)

    def add_slot(slot, acc):
        row_start = offs[slot, 0]
        col_start = offs[slot, 1]
        piece = lax.dynamic_index_in_dim(pieces, slot, 0, keepdims=False)
        current = lax.dynamic_slice(acc, (zero_index, row_start, col_start), (3, frame, frame))
        return lax.dynamic_update_slice(acc, current + piece, (zero_index, row_start, col_start))

    acc = jnp.zeros((3, tile + frame, tile + frame), jnp.float32)
    acc = lax.fori_loop(0, slots, add_slot, acc)
    grad_re = win_re * chi_re + win_im * chi_im
    grad_im = win_re * chi_im - win_im * chi_re
    slot_grad = jnp.stack([grad_re, grad_im])
    spilled = from_behind(acc[:, :, tile:], "ty", 1)
    merged = acc[:, :, :tile].at[:, :, :frame].add(spilled)
    dropped = from_behind(merged[:, tile:, :], "tx", 1)
    totals = merged[:, :tile, :].at[:, :frame, :].add(dropped)
    local_illum = jnp.sum(totals[2])
    norms, illum_sum = lax.psum((local_norms, local_illum), ("tx", "ty"))
    cells = lax.axis_size("tx") * lax.axis_size("ty") * tile * tile
    mean_illum = illum_sum / cells
    new_object = obj_field + totals[:2] / (totals[2] + mean_illum)[None]
    flat_rows = 2 * modes * frame
    flat_eig = eig32.reshape(flat_rows, frame)
    gprobe = jnp.einsum("sk,csij->ckij", wts, slot_grad, precision=high)
    flat_grad = gprobe.reshape(flat_rows, frame)
    share_rows = flat_rows // (lax.axis_size("tx") * lax.axis_size("ty"))
    start = lax.axis_index(("tx", "ty")) * share_rows
    share = lax.psum_scatter(flat_grad, ("tx", "ty"), scatter_dimension=0, tiled=True)
    own = lax.dynamic_slice_in_dim(flat_eig, start, share_rows, 0)
    updated = own + share / row_divisor(norms, start, share_rows, frame, modes)[:, None]
    new_eig = lax.all_gather(updated, ("tx", "ty"), axis=0, tiled=True).reshape(
        2, modes, frame, frame
    )
    return (new_object, new_eig)


def solution(mesh):
    return jax.shard_map(
        per_device,
        mesh=mesh,
        in_specs=(
            P(None, ("grp", "tx"), "ty"),
            P(None, "grp", None, None),
            P(("grp", "tx"), "ty", None, None),
            P(("grp", "tx"), "ty", None, None),
            P(("grp", "tx"), "ty"),
            P(("grp", "tx"), "ty", None, None, None),
        ),
        out_specs=(P(None, ("grp", "tx"), "ty"), P(None, "grp", None, None)),
        check_vma=False,
    )
```

profile of v0, /device:TPU:0, one launch (start us, length us, event | category | flops | bytes accessed | tf_op | source)
XLA Modules:
  0.0 175.8 jit_solution(10866427820670619271)
XLA Ops:
  7.2 5.1 %collective-permute-start = (f32[2,128,128]{2,1,0:T(8,128)}, f32[2,128,128]{2,1,0:T(8,128)S(1)}, u32[]{:S(2)}, u32[]{:S(2)}) collective-permute-start(f32[2,128,128]{2,1,0:T(8,128)} %param.16), channel_id=1, source_target_pairs={{0,12},{4,0},{8,4},{12,8},{1,13},{5,1},{9,5},{13,9},{2,14},{6,2},{... | collective-permute-start | bytes 393224 | tf_op jit(solution)/shard_map/ppermute | solution.py:14
  13.0 0.8 compare_select_fusion.1
  13.9 0.9 constant_dynamic-update-slice_fusion.1
  15.6 2.2 %convolution_bitcast_fusion.1 = f32[2,3,128,128]{3,1,2,0:T(4,128)S(1)} fusion(bf16[2,16,128,128]{3,2,1,0:T(8,128)(2,1)} %param.17, f32[1,1,3,16]{3,1,2,0:T(1,128)} %param.18), kind=kOutput, calls=%fused_computation.7 | convolution fusion | flops 18874368 | bytes 1441984 | tf_op jit(solution)/shard_map/sk,ckij->csij/dot_general | solution.py:69
  17.8 1.7 collective-permute-done.1
  19.5 15.2 %while.19 = (s32[]{:T(128)}, f32[2,256,256]{2,1,0:T(8,128)S(1)}, s32[3,3]{1,0:T(4,128)S(1)}, f32[3,2,128,128]{3,0,2,1:T(4,128)S(1)}, s32[]{:T(128)}, /*index=5*/s32[]{:T(128)}) while((s32[]{:T(128)}, f32[2,256,256]{2,1,0:T(8,128)S(1)}, s32[3,3]{1,0:T(4,128)S(1)}, f32[3,2,128,128]{3,0,2,1:T(4,128)S(1)}, s32[]{:T(128)}, /*index=5*/s32[]{:T(128)}) %tuple.75), condition=%wide.while_cond.2, body=%wide.while_body.2.sunk | while | flops 2 | bytes 524421 | solution.py:63
  20.1 1.3 constant_dynamic-slice_fusion.12
  21.4 3.1 %dynamic-update-slice.11 = f32[3,2,128,128]{3,0,2,1:T(4,128)S(1)} dynamic-update-slice(f32[3,2,128,128]{3,0,2,1:T(4,128)S(1)} %get-tuple-element.253, f32[1,2,128,128]{3,0,2,1:T(1,128)S(1)} %bitcast.173, s32[]{:T(128)S(6)} %copy.157, s32[]{:T(128)} %constant.159.clone.1..sunk.1, s32[]{:T(128)} %constant.159.clone.1..sunk.1, s32[]{:T(128)} %constant.159.clone.1..sunk.1) | dynamic-update-slice | bytes 262148 | tf_op jit(solution)/shard_map/vmap()/gather
  25.1 1.3 constant_dynamic-slice_fusion.12
  26.4 3.1 %dynamic-update-slice.11 = f32[3,2,128,128]{3,0,2,1:T(4,128)S(1)} dynamic-update-slice(f32[3,2,128,128]{3,0,2,1:T(4,128)S(1)} %get-tuple-element.253, f32[1,2,128,128]{3,0,2,1:T(1,128)S(1)} %bitcast.173, s32[]{:T(128)S(6)} %copy.157, s32[]{:T(128)} %constant.159.clone.1..sunk.1, s32[]{:T(128)} %constant.159.clone.1..sunk.1, s32[]{:T(128)} %constant.159.clone.1..sunk.1) | dynamic-update-slice | bytes 262148 | tf_op jit(solution)/shard_map/vmap()/gather
  30.1 1.3 constant_dynamic-slice_fusion.12
  31.4 3.1 %dynamic-update-slice.11 = f32[3,2,128,128]{3,0,2,1:T(4,128)S(1)} dynamic-update-slice(f32[3,2,128,128]{3,0,2,1:T(4,128)S(1)} %get-tuple-element.253, f32[1,2,128,128]{3,0,2,1:T(1,128)S(1)} %bitcast.173, s32[]{:T(128)S(6)} %copy.157, s32[]{:T(128)} %constant.159.clone.1..sunk.1, s32[]{:T(128)} %constant.159.clone.1..sunk.1, s32[]{:T(128)} %constant.159.clone.1..sunk.1) | dynamic-update-slice | bytes 262148 | tf_op jit(solution)/shard_map/vmap()/gather
  40.0 0.7 fusion.39
  40.8 0.7 fusion.43
  41.5 0.8 fusion
  43.6 0.7 fusion.1
  46.3 2.1 %convolution_bitcast_fusion = f32[2,16,128,128]{3,1,2,0:T(8,128)S(1)} fusion(f32[1,3,128,128]{3,1,2,0:T(4,128)S(1)} %get-tuple-element.177, f32[1,3,128,128]{3,1,2,0:T(4,128)S(1)} %get-tuple-element.176, f32[1,1,3,16]{3,1,2,0:T(1,128)S(1)} %copy-done.3), kind=kOutput, calls=%fused_computation.6 | convolution fusion | flops 18972672 | bytes 2490560 | tf_op jit(solution)/shard_map/sk,csij->ckij/dot_general | solution.py:108
  48.4 1.9 %copy.84 = f32[2,16,128,128]{3,2,1,0:T(8,128)} copy(f32[2,16,128,128]{3,1,2,0:T(8,128)S(1)} %convolution_bitcast_fusion) | data formatting | bytes 4194304 | tf_op jit(solution)/shard_map/sk,csij->ckij/transpose | solution.py:108
  51.1 23.3 %while.18 = (s32[]{:T(128)}, f32[3,256,256]{2,1,0:T(8,128)S(1)}, s32[3,2]{0,1:T(2,128)S(1)}, f32[3,3,128,128]{3,0,2,1:T(4,128)S(1)}, s32[]{:T(128)}, /*index=5*/s32[]{:T(128)}, s32[]{:T(128)}) while((s32[]{:T(128)}, f32[3,256,256]{2,1,0:T(8,128)S(1)}, s32[3,2]{0,1:T(2,128)S(1)}, f32[3,3,128,128]{3,0,2,1:T(4,128)S(1)}, s32[]{:T(128)}, ...), condition=%wide.region_1.2_spmd, body=%wide.region_0.0_spmd.sunk | while | flops 49160 | bytes 1376445 | solution.py:93
  51.3 0.7 constant_dynamic-slice_fusion.10
  55.8 3.0 %dynamic_update_slice.8 = f32[3,256,256]{2,1,0:T(8,128)S(1)} dynamic-update-slice(f32[3,256,256]{2,1,0:T(8,128)S(1)} %get-tuple-element.270, f32[3,128,128]{2,1,0:T(8,128)S(1)} %dynamic-slice_add_fusion.2, s32[]{:T(128)} %constant.159.clone.1..sunk, s32[]{:T(128)S(6)} %select_n.170, s32[]{:T(128)S(6)} %select_n.171) | dynamic-update-slice | bytes 393220 | tf_op jit(solution)/shard_map/while/body/eval_jaxpr/dynamic_update_slice | solution.py:90
  59.1 0.7 constant_dynamic-slice_fusion.10
  63.6 3.0 %dynamic_update_slice.8 = f32[3,256,256]{2,1,0:T(8,128)S(1)} dynamic-update-slice(f32[3,256,256]{2,1,0:T(8,128)S(1)} %get-tuple-element.270, f32[3,128,128]{2,1,0:T(8,128)S(1)} %dynamic-slice_add_fusion.2, s32[]{:T(128)} %constant.159.clone.1..sunk, s32[]{:T(128)S(6)} %select_n.170, s32[]{:T(128)S(6)} %select_n.171) | dynamic-update-slice | bytes 393220 | tf_op jit(solution)/shard_map/while/body/eval_jaxpr/dynamic_update_slice | solution.py:90
  71.4 3.0 %dynamic_update_slice.8 = f32[3,256,256]{2,1,0:T(8,128)S(1)} dynamic-update-slice(f32[3,256,256]{2,1,0:T(8,128)S(1)} %get-tuple-element.270, f32[3,128,128]{2,1,0:T(8,128)S(1)} %dynamic-slice_add_fusion.2, s32[]{:T(128)} %constant.159.clone.1..sunk, s32[]{:T(128)S(6)} %select_n.170, s32[]{:T(128)S(6)} %select_n.171) | dynamic-update-slice | bytes 393220 | tf_op jit(solution)/shard_map/while/body/eval_jaxpr/dynamic_update_slice | solution.py:90
  74.5 1.1 collective-permute-start.2
  75.6 6.1 %collective-permute-done.2 = f32[3,256,128]{2,1,0:T(8,128)S(1)} collective-permute-done((f32[3,256,128]{2,1,0:T(8,128)S(1)}, f32[3,256,128]{2,1,0:T(8,128)S(1)}, u32[]{:S(2)}, u32[]{:S(2)}) %collective-permute-start.2) | collective-permute-done | bytes 393248 | tf_op jit(solution)/shard_map/ppermute | solution.py:14
  82.2 11.8 %collective-permute-done.3 = f32[3,128,128]{2,1,0:T(8,128)S(1)} collective-permute-done((f32[3,128,128]{2,1,0:T(8,128)S(1)}, f32[3,128,128]{2,1,0:T(8,128)S(1)}, u32[]{:S(2)}, u32[]{:S(2)}) %collective-permute-start.3) | collective-permute-done | bytes 196640 | tf_op jit(solution)/shard_map/ppermute | solution.py:14
  94.7 30.5 %all-reduce = (f32[]{:T(128)}, f32[16]{0:T(128)S(1)}) all-reduce(f32[]{:T(128)} %slice_reduce_fusion, f32[16]{0:T(128)S(1)} %fusion.80), channel_id=1, replica_groups=mesh['grp'=2,'tx'=4,'ty'=4] {'tx','ty'}, use_global_device_ids=true, to_apply=%region_3.4 | all-reduce | flops 17 | bytes 136 | tf_op jit(solution)/shard_map/psum | solution.py:102
  125.3 1.7 convert_add_fusion
  127.7 0.7 fusion.22
  128.4 37.5 %all-gather.2.cloned.1.call-done = f32[4096,128]{1,0:T(8,128)} async-done(((f32[256,128]{1,0:T(8,128)}), f32[4096,128]{1,0:T(8,128)}) %all-gather.2.cloned.1.call-update) | async-done | bytes 2097168 | tf_op jit(solution)/shard_map/all_gather | solution.py:115
  165.9 3.1 %copy.169 = f32[2,16,128,128]{3,2,1,0:T(8,128)} copy(f32[2,16,128,128]{3,2,1,0:T(8,128)} %bitcast.175) | data formatting | bytes 4194304
  (65 shorter events, 14.7 us)
Async XLA Ops:
  7.2 118.1 %reduce-scatter.2.cloned.1.call-start = ((), (), s32[]{:S(2)}) async-start(), calls=%async_computation.1 | async-start | bytes 2228224 | tf_op jit(solution)/shard_map/reduce_scatter | solution.py:112
  7.2 8.2 %collective-permute-start = (f32[2,128,128]{2,1,0:T(8,128)}, f32[2,128,128]{2,1,0:T(8,128)S(1)}, u32[]{:S(2)}, u32[]{:S(2)}) collective-permute-start(f32[2,128,128]{2,1,0:T(8,128)} %param.16), channel_id=1, source_target_pairs={{0,12},{4,0},{8,4},{12,8},{1,13},{5,1},{9,5},{13,9},{2,14},{6,2},{... | collective-permute-start | bytes 393224 | tf_op jit(solution)/shard_map/ppermute | solution.py:14
  15.4 4.0 %collective-permute-start.1 = (f32[2,256,128]{2,1,0:T(8,128)S(1)}, f32[2,256,128]{2,1,0:T(8,128)S(1)}, u32[]{:S(2)}, u32[]{:S(2)}) collective-permute-start(f32[2,256,128]{2,1,0:T(8,128)S(1)} %constant_dynamic-update-slice_fusion), channel_id=1, source_target_pairs={{0,3},{1,0},{2,1},{3,2},{4,7},{5,4},{6,5},{7,6},{8,11},{9,8},{10,9... | collective-permute-start | bytes 786440 | tf_op jit(solution)/shard_map/ppermute | solution.py:14
  35.5 4.5 %copy-start.1 = (bf16[1,1,3,128,128]{4,3,2,1,0:T(8,128)(2,1)S(1)}, bf16[1,1,3,128,128]{4,3,2,1,0:T(8,128)(2,1)}, u32[]{:S(2)}) copy-start(bf16[1,1,3,128,128]{4,3,2,1,0:T(8,128)(2,1)} %param.21) | copy-start | bytes 294916
  43.6 2.7 %copy-start.3 = (f32[1,1,3,16]{3,1,2,0:T(1,128)S(1)}, f32[1,1,3,16]{3,1,2,0:T(1,128)}, u32[]{:S(2)}) copy-start(f32[1,1,3,16]{3,1,2,0:T(1,128)} %param.18) | copy-start | bytes 580
  50.4 0.7 copy-start.2
  50.4 115.5 %all-gather.2.cloned.1.call-start = ((), (), s32[]{:S(2)}) async-start(), calls=%async_computation.2 | async-start | bytes 2228224 | tf_op jit(solution)/shard_map/all_gather | solution.py:115
  74.4 53.3 %copy-start = (f32[2,128,128]{2,1,0:T(8,128)S(1)}, f32[2,128,128]{2,1,0:T(8,128)}, u32[]{:S(2)}) copy-start(f32[2,128,128]{2,1,0:T(8,128)} %param.16) | copy-start | bytes 393220
  74.5 7.3 %collective-permute-start.2 = (f32[3,256,128]{2,1,0:T(8,128)S(1)}, f32[3,256,128]{2,1,0:T(8,128)S(1)}, u32[]{:S(2)}, u32[]{:S(2)}) collective-permute-start(f32[3,256,128]{2,1,0:T(8,128)S(1)} %slice.92), channel_id=1, source_target_pairs={{0,1},{1,2},{2,3},{3,0},{4,5},{5,6},{6,7},{7,4},{8,9},{9,10},{10,1... | collective-permute-start | bytes 1179656 | tf_op jit(solution)/shard_map/ppermute | solution.py:14
  81.8 12.3 %collective-permute-start.3 = (f32[3,128,128]{2,1,0:T(8,128)S(1)}, f32[3,128,128]{2,1,0:T(8,128)S(1)}, u32[]{:S(2)}, u32[]{:S(2)}) collective-permute-start(f32[3,128,128]{2,1,0:T(8,128)S(1)} %slice.115), channel_id=1, source_target_pairs={{0,4},{4,8},{8,12},{12,0},{1,5},{5,9},{9,13},{13,1},{2,6},{6,10},{... | collective-permute-start | bytes 589832 | tf_op jit(solution)/shard_map/ppermute | solution.py:14
Sparse Core Ops, SparseCore 0:
  50.5 65.2 reduce-scatter.1
  127.1 38.7 all-gather.1
where the time goes:
time: 177 us; the launch traced here: 176 us
  waiting for transfers between devices  57.8 us (33%)
  local copies, waits for them, and re-layouts  33.1 us (19%)
  blocking collectives  30.5 us (17%)
  between operations  15.7 us (9%)
  matrix products  14.7 us (8%)
  loops' own time  11.7 us (7%)
  starting transfers between devices  6.8 us (4%)
  other arithmetic  5.48 us (3%)
    all_gather x1, waiting for transfers between devices, per_device(): lax.all_gather(updated, ('tx', 'ty'), axis=0, tiled=True)  37.5 us
    psum x1, blocking collectives, per_device(): norms, illum_sum = lax.psum((local_norms, local_illum), ('tx', 'ty'))  30.5 us
    ppermute x4, waiting for transfers between devices, from_behind(): return lax.ppermute(value, axis, pairs)  20.2 us
    gather x12, local copies, waits for them, and re-layouts  14.9 us
    another operation x1, loops' own time, per_device(): acc = lax.fori_loop(0, slots, add_slot, acc)  11.4 us
    dynamic_update_slice x3, local copies, waits for them, and re-layouts, add_slot(): lax.dynamic_update_slice(acc, current + piece, (zero_index, row_start, co...  9.01 us
    ppermute x4, starting transfers between devices, from_behind(): return lax.ppermute(value, axis, pairs)  6.72 us
    unnamed x11, local copies, waits for them, and re-layouts  4.42 us
  transfers between devices with their start and end apart: 6, of which 5 were waited for; matrix products, arithmetic and copies ran while one was open for 10% of the time, Pallas kernels for 0%

commit v1 on v0

--- a/solution.py
+++ b/solution.py
@@ -1,9 +1,15 @@
+import functools
 import math
 
 import jax
 import jax.numpy as jnp
+import numpy as np
 from jax import lax
+from jax.experimental import pallas as pl
+from jax.experimental.pallas import tpu as pltpu
 from jax.sharding import PartitionSpec as P
+
+MESH = pl.DeviceIdType.MESH
 
 high = lax.Precision.HIGHEST
 
@@ -118,9 +124,368 @@
     return (new_object, new_eig)
 
 
+def dft_tables(frame):
+    grid = np.arange(frame)
+    angle = (grid[:, None] * grid[None, :] % frame) * (2.0 * math.pi / frame)
+    re = np.cos(angle) / math.sqrt(frame)
+    im = -np.sin(angle) / math.sqrt(frame)
+    right = np.block([[re, im], [-im, re]]).astype(np.float32)
+    return right, np.ascontiguousarray(right.T)
+
+
+def dot(a, b):
+    return jnp.dot(a, b, precision=high, preferred_element_type=jnp.float32)
+
+
+def fused_kernel(
+    ntx, nty, w_s, off_s, cnt_s, obj, eig, w_v, amps, tab_r, tab_l, out_obj, out_eig,
+    below, right, diag, probe, win, acc, in_right, in_diag, in_below, msg, msg_all, grads, grads_all, upd,
+    halo_ss, halo_rs, msg_ss, msg_rs, a2a_ss, a2a_rs, sp_ss, sp_rs, gat_ss, gat_rs,
+):
+    frame = eig.shape[2]
+    modes = eig.shape[1]
+    slots = amps.shape[0]
+    n = ntx * nty
+    nx = nty // 2
+    share = 2 * frame // n
+    unit = slots * share
+    mrows = msg.shape[0]
+    tx = lax.axis_index("tx")
+    ty = lax.axis_index("ty")
+    me = tx * nty + ty
+    peers = [(a, b) for a in range(ntx) for b in range(nty) if (a, b) != (0, 0)]
+
+    def at(a, b):
+        return {"tx": lax.rem(tx + (a + ntx), ntx), "ty": lax.rem(ty + (b + nty), nty)}
+
+    def send(src, dst, ss, rs, where):
+        copy = pltpu.make_async_remote_copy(
+            src_ref=src, dst_ref=dst, send_sem=ss, recv_sem=rs, device_id=where, device_id_type=MESH
+        )
+        copy.start()
+        return copy
+
+    barrier = pltpu.get_barrier_semaphore()
+    for a, b in peers:
+        pl.semaphore_signal(barrier, inc=1, device_id=at(a, b), device_id_type=MESH)
+    pl.semaphore_wait(barrier, n - 1)
+
+    halo = []
+    for c in range(2):
+        halo.append(send(obj.at[c], below.at[c], halo_ss.at[c], halo_rs.at[c], at(-1, 0)))
+    for c in range(2):
+        halo.append(send(obj.at[c], right.at[c], halo_ss.at[2 + c], halo_rs.at[2 + c], at(0, -1)))
+
+    lives = [jnp.where(s < cnt_s[0], jnp.float32(1.0), jnp.float32(0.0)) for s in range(slots)]
+    step = 32
+
+    def probe_rows(i, total):
+        rows = pl.ds(pl.multiple_of(i * step, step), step)
+        parts = [[None, None] for _ in range(slots)]
+        for k in range(modes):
+            for c in range(2):
+                e = eig[c, k, rows, :].astype(jnp.float32)
+                for s in range(slots):
+                    term = w_s[s * modes + k] * e
+                    parts[s][c] = term if k == 0 else parts[s][c] + term
+        for s in range(slots):
+            probe[s, 0, rows, :] = parts[s][0]
+            probe[s, 1, rows, :] = parts[s][1]
+            power = (parts[s][0] * parts[s][0] + parts[s][1] * parts[s][1]) * lives[s]
+            total = total + jnp.sum(power, axis=0, keepdims=True)
+        return total
+
+    total = lax.fori_loop(0, frame // step, probe_rows, jnp.zeros((1, frame), jnp.float32))
+
+    msg[...] = jnp.zeros_like(msg)
+    wv = w_v[...]
+    slot_id = lax.broadcasted_iota(jnp.int32, wv.shape, 0)
+    msg[0:slots, 0:modes] = wv
+    msg[slots : 2 * slots, 0:modes] = jnp.where(slot_id < cnt_s[0], wv * wv, 0.0)
+    msg[2 * slots : 2 * slots + 1, :] = total
+    mine = pl.ds(pl.multiple_of(me * mrows, mrows), mrows)
+    msg_all[mine, :] = msg[...]
+    msgs = [
+        send(msg, msg_all.at[mine], msg_ss.at[q], msg_rs.at[q], at(a, b)) for q, (a, b) in enumerate(peers)
+    ]
+
+    lane = lax.broadcasted_iota(jnp.int32, (frame, frame), 1)
+    row = lax.broadcasted_iota(jnp.int32, (frame, frame), 0)
+    starts = [(off_s[2 * s], off_s[2 * s + 1]) for s in range(slots)]
+
+    def spread(channel, piece_of):
+        quads = [None] * 4
+        for s in range(slots):
+            r, c = starts[s]
+            moved = pltpu.roll(pltpu.roll(piece_of(s), r, 0), c, 1)
+            top, left = row >= r, lane >= c
+            upper = jnp.where(top, moved, 0.0)
+            lower = jnp.where(top, 0.0, moved)
+            cut = [
+                jnp.where(left, upper, 0.0), jnp.where(left, 0.0, upper),
+                jnp.where(left, lower, 0.0), jnp.where(left, 0.0, lower),
+            ]
+            quads = [x if q is None else q + x for q, x in zip(quads, cut)]
+        for q in range(4):
+            acc[q, channel] = quads[q]
+
+    spill = [None] * 9
+
+    def push_right(channel):
+        to = at(0, 1)
+        spill[channel] = send(
+            acc.at[3, channel], in_diag.at[channel], sp_ss.at[channel], sp_rs.at[channel], to
+        )
+        k = 3 + channel
+        spill[k] = send(acc.at[1, channel], in_right.at[channel], sp_ss.at[k], sp_rs.at[k], to)
+
+    def push_down(channel):
+        spill[channel].wait_recv()
+        acc[2, channel] = acc[2, channel] + in_diag[channel]
+        k = 6 + channel
+        spill[k] = send(acc.at[2, channel], in_below.at[channel], sp_ss.at[k], sp_rs.at[k], at(1, 0))
+
+    spread(2, lambda s: (probe[s, 0] * probe[s, 0] + probe[s, 1] * probe[s, 1]) * lives[s])
+
+    for c in range(2):
+        halo[c].wait_recv()
+        halo.append(send(below.at[c], diag.at[c], halo_ss.at[4 + c], halo_rs.at[4 + c], at(0, -1)))
+    push_right(2)
+    for c in range(2):
+        halo[2 + c].wait_recv()
+    for c in range(2):
+        halo[4 + c].wait_recv()
+
+    for s in range(slots):
+        r, c = starts[s]
+        top, left = row >= r, lane >= c
+        back_r, back_c = lax.rem(frame - r, frame), lax.rem(frame - c, frame)
+        for z in range(2):
+            picked = jnp.where(
+                top, jnp.where(left, obj[z], right[z]), jnp.where(left, below[z], diag[z])
+            )
+            win[s, z] = pltpu.roll(pltpu.roll(picked, back_r, 0), back_c, 1)
+
+    stacked = jnp.concatenate(
+        [
+            jnp.concatenate(
+                [
+                    probe[s, 0] * win[s, 0] - probe[s, 1] * win[s, 1],
+                    probe[s, 0] * win[s, 1] + probe[s, 1] * win[s, 0],
+                ],
+                axis=1,
+            )
+            for s in range(slots)
+        ],
+        axis=0,
+    )
+    half = dot(stacked, tab_r[...])
+    upright = jnp.concatenate(
+        [
+            jnp.concatenate(
+                [half[s * frame : (s + 1) * frame, :frame], half[s * frame : (s + 1) * frame, frame:]], axis=0
+            )
+            for s in range(slots)
+        ],
+        axis=1,
+    )
+    spec = dot(tab_l[...], upright)
+    scaled = []
+    for s in range(slots):
+        re = spec[:frame, s * frame : (s + 1) * frame]
+        im = spec[frame:, s * frame : (s + 1) * frame]
+        factor = (amps[s].astype(jnp.float32) / jnp.sqrt(re * re + im * im + 0.25) - 1.0) * lives[s]
+        scaled.append(jnp.concatenate([re * factor, im * factor], axis=0))
+    half = dot(tab_r[...], jnp.concatenate(scaled, axis=1))
+    flat = jnp.concatenate(
+        [
+            jnp.concatenate(
+                [half[:frame, s * frame : (s + 1) * frame], half[frame:, s * frame : (s + 1) * frame]], axis=1
+            )
+            for s in range(slots)
+        ],
+        axis=0,
+    )
+    chi = dot(flat, tab_l[...])
+    chis = [
+        (chi[s * frame : (s + 1) * frame, :frame], chi[s * frame : (s + 1) * frame, frame:]) for s in range(slots)
+    ]
+
+    for s in range(slots):
+        chi_re, chi_im = chis[s]
+        pair = (
+            win[s, 0] * chi_re + win[s, 1] * chi_im,
+            win[s, 0] * chi_im - win[s, 1] * chi_re,
+        )
+        for i in range(n):
+            z, start = divmod(i * share, frame)
+            at_row = (i * slots + s) * share
+            grads[at_row : at_row + share, :] = pair[z][start : start + share, :]
+    block = pl.ds(pl.multiple_of(me * unit, unit), unit)
+    swaps = []
+    for q, (a, b) in enumerate(peers):
+        to = at(a, b)
+        theirs = pl.ds(pl.multiple_of((to["tx"] * nty + to["ty"]) * unit, unit), unit)
+        swaps.append(send(grads.at[theirs], grads_all.at[block], a2a_ss.at[q], a2a_rs.at[q], to))
+    grads_all[block, :] = grads[block, :]
+
+    spread(0, lambda s: probe[s, 0] * chis[s][0] + probe[s, 1] * chis[s][1])
+    push_right(0)
+    spread(1, lambda s: probe[s, 0] * chis[s][1] - probe[s, 1] * chis[s][0])
+    push_right(1)
+    push_down(2)
+    push_down(0)
+    push_down(1)
+
+    for copy in msgs:
+        copy.wait_recv()
+    pick = [msg_all[pl.ds(s, n, stride=mrows), :] for s in range(2 * slots)]
+    mix = jnp.concatenate(pick[:slots], axis=0).T[:modes, :]
+    squares = sum(pick[slots:])
+    norms = dot(squares.T[:modes, :], jnp.ones((n, frame), jnp.float32))
+    inverse = 1.0 / (norms + 1.0)
+    mean = jnp.sum(msg_all[pl.ds(2 * slots, n, stride=mrows), :]) / (n * frame * frame)
+
+    for copy in swaps:
+        copy.wait_recv()
+    wide = jnp.concatenate(
+        [
+            jnp.concatenate(
+                [grads_all[pl.ds(s * share + r, n, stride=unit), :] for s in range(slots)], axis=0
+            )
+            for r in range(share)
+        ],
+        axis=1,
+    )
+    moved = dot(mix, wide)
+    for r in range(share):
+        upd[pl.ds(r, modes, stride=share), :] = moved[:, r * frame : (r + 1) * frame] * inverse
+
+    def place(i):
+        flat_row = i * share
+        return (flat_row // frame, pl.multiple_of(lax.rem(flat_row, frame), share))
+
+    def rows_of(a, b):
+        to = at(a, b)
+        z, start = place(to["tx"] * nty + to["ty"])
+        return out_eig.at[z, :, pl.ds(start, share), :]
+
+    z, start = place(me)
+    own = eig[z, :, pl.ds(start, share), :].astype(jnp.float32)
+    out_eig[z, :, pl.ds(start, share), :] = own + upd[...].reshape(modes, share, frame)
+
+    core = lax.rem(ty, 2)
+    ty_of = lambda j: lax.rem(ty + 2 * j, nty)
+    other = {"tx": tx, "ty": ty + 1 - 2 * core}
+
+    def gathered(d, j):
+        z, start = place(lax.rem(tx - d + ntx, ntx) * nty + lax.rem(ty - 2 * j + nty, nty))
+        return out_eig.at[z, :, pl.ds(start, share), :]
+
+    def pass_on(d, j, kind, to):
+        ref = gathered(d, j)
+        k = (kind * ntx + d) * nx + j
+        return send(ref, ref, gat_ss.at[k], gat_rs.at[k], to)
+
+    along = {}
+    across = {}
+    over = []
+
+    def hop(ref, kind, d, j, to):
+        k = (kind * ntx + d) * nx + j
+        return send(ref, ref, gat_ss.at[k], gat_rs.at[k], to)
+
+    for d in range(1, ntx):
+        along[d] = hop(gathered(0, 0), 0, d, 0, at(d, 0))
+    for j in range(1, nx):
+        across[0, j] = hop(gathered(0, 0), 1, 0, j, at(0, 2 * j))
+    over.append(hop(gathered(0, 0), 2, 0, 0, other))
+    for d in range(1, ntx):
+        along[d].wait_recv()
+        for j in range(1, nx):
+            across[d, j] = hop(gathered(d, 0), 1, d, j, at(0, 2 * j))
+        over.append(hop(gathered(d, 0), 2, d, 0, other))
+
+    for k in range(3, 9):
+        spill[k].wait_recv()
+    illum = acc[0, 2] + in_right[2] + in_below[2] + mean
+    for c in range(2):
+        out_obj[c] = obj[c] + (acc[0, c] + in_right[c] + in_below[c]) / illum
+
+    for d in range(ntx):
+        for j in range(1, nx):
+            across[d, j].wait_recv()
+            over.append(hop(gathered(d, j), 2, d, j, other))
+    for copy in over:
+        copy.wait_recv()
+    for copy in halo + msgs + swaps + spill + list(along.values()) + list(across.values()) + over:
+        copy.wait_send()
+
+
+def per_device_fused(mesh, obj_field, eigenprobes, weights, offsets, counts, amplitudes):
+    ntx, nty = mesh.shape["tx"], mesh.shape["ty"]
+    n = ntx * nty
+    tile, width = obj_field.shape[1:]
+    _, modes, frame, _ = eigenprobes.shape
+    slots = weights.shape[2]
+    fits = tile == width == frame and frame % 128 == 0 and nty % 2 == 0 and n % 8 == 0
+    if not (fits and (2 * frame) % (16 * n) == 0 and frame % (2 * frame // n) == 0):
+        return per_device(obj_field, eigenprobes, weights, offsets, counts, amplitudes)
+    share = 2 * frame // n
+    mrows = -(-(2 * slots + 1) // 8) * 8
+    tab_r, tab_l = dft_tables(frame)
+    vmem = pl.BlockSpec(memory_space=pltpu.VMEM)
+    smem = pl.BlockSpec(memory_space=pltpu.SMEM)
+    nx = nty // 2
+    f32 = jnp.float32
+    square = (frame, frame)
+    dma = pltpu.SemaphoreType.DMA
+    return tuple(pl.pallas_call(
+        functools.partial(fused_kernel, ntx, nty),
+        out_shape=(
+            jax.ShapeDtypeStruct(obj_field.shape, f32),
+            jax.ShapeDtypeStruct(eigenprobes.shape, f32),
+        ),
+        in_specs=[smem] * 3 + [vmem] * 6,
+        out_specs=(vmem, vmem),
+        scratch_shapes=[
+            pltpu.VMEM((2,) + square, f32),
+            pltpu.VMEM((2,) + square, f32),
+            pltpu.VMEM((2,) + square, f32),
+            pltpu.VMEM((slots, 2) + square, f32),
+            pltpu.VMEM((slots, 2) + square, f32),
+            pltpu.VMEM((4, 3) + square, f32),
+            pltpu.VMEM((3,) + square, f32),
+            pltpu.VMEM((3,) + square, f32),
+            pltpu.VMEM((3,) + square, f32),
+            pltpu.VMEM((mrows, frame), f32),
+            pltpu.VMEM((n * mrows, frame), f32),
+            pltpu.VMEM((n * slots * share, frame), f32),
+            pltpu.VMEM((n * slots * share, frame), f32),
+            pltpu.VMEM((modes * share, frame), f32),
+            dma((6,)), dma((6,)),
+            dma((n - 1,)), dma((n - 1,)),
+            dma((n - 1,)), dma((n - 1,)),
+            dma((9,)), dma((9,)),
+            dma((3 * ntx * nx,)), dma((3 * ntx * nx,)),
+        ],
+        compiler_params=pltpu.CompilerParams(collective_id=0, has_side_effects=True),
+    )(
+        weights.reshape(slots * modes),
+        offsets.reshape(slots * 2),
+        counts.reshape(1),
+        obj_field,
+        eigenprobes,
+        weights.reshape(slots, modes),
+        amplitudes.reshape((slots,) + square),
+        jnp.asarray(tab_r),
+        jnp.asarray(tab_l),
+    ))
+
+
 def solution(mesh):
     return jax.shard_map(
-        per_device,
+        functools.partial(per_device_fused, mesh),
         mesh=mesh,
         in_specs=(
             P(None, ("grp", "tx"), "ty"),

time: 177 us -> 60.9 us (0.34)
  waiting for transfers between devices: 57.8 us -> 0 us
  Pallas kernels: 0 us -> 50.1 us
  blocking collectives: 30.5 us -> 0 us
  local copies, waits for them, and re-layouts: 33.1 us -> 7.98 us
  matrix products: 14.7 us -> 0 us
  between operations: 15.7 us -> 1.29 us
  loops' own time: 11.7 us -> 0 us
  starting transfers between devices: 6.8 us -> 0 us
  other arithmetic: 5.48 us -> 0.7 us
    pallas_call x0 -> x1, Pallas kernels: none -> 50.1 us  [per_device_fused(): pl.pallas_call(functools.partial(fused_kernel, ntx, nty), out_shape=(jax....]
    all_gather x1 -> x0, waiting for transfers between devices: 37.5 us -> none  [per_device(): lax.all_gather(updated, ('tx', 'ty'), axis=0, tiled=True)]
    psum x1 -> x0, blocking collectives: 30.5 us -> none  [per_device(): norms, illum_sum = lax.psum((local_norms, local_illum), ('tx', 'ty'))]
    ppermute x4 -> x0, waiting for transfers between devices: 20.2 us -> none  [from_behind(): return lax.ppermute(value, axis, pairs)]
    gather x12 -> x0, local copies, waits for them, and re-layouts: 14.9 us -> none
    dot_general x18 -> x0, matrix products: 14.7 us -> none  [the longest x1 2.2 us: per_device(): probe = jnp.einsum('sk,ckij->csij', wts, eig32, precision=high)]
    another operation x2 -> x0, loops' own time: 11.7 us -> none  [the longest x1 11.4 us: per_device(): acc = lax.fori_loop(0, slots, add_slot, acc)]
    dynamic_update_slice x3 -> x0, local copies, waits for them, and re-layouts: 9.01 us -> none  [add_slot(): lax.dynamic_update_slice(acc, current + piece, (zero_index, row_start, co...]
  transfers between devices with their start and end apart: 6 -> 0, of which waited for: 5 -> 0; matrix products, arithmetic and copies ran while one was open for 10% -> 0% of each run, Pallas kernels for 0% -> 0%
where the time goes in v1:
time: 60.9 us; the launch traced here: 60.1 us
  Pallas kernels  50.1 us (82%)
  local copies, waits for them, and re-layouts  7.98 us (13%)
  between operations  1.29 us (2%)
  other arithmetic  0.7 us (1%)
    pallas_call x1, Pallas kernels, per_device_fused(): pl.pallas_call(functools.partial(fused_kernel, ntx, nty), out_shape=(jax....  50.1 us
    unnamed x4, local copies, waits for them, and re-layouts  6.73 us

profile of v1, /device:TPU:0, one launch (start us, length us, event | category | flops | bytes accessed | tf_op | source)
XLA Modules:
  0.0 60.1 jit_solution(7192553488802114528)
XLA Ops:
  1.3 0.8 %copy.11 = s32[1,1,3,2]{3,2,1,0:T(4,128)S(1)} copy(s32[1,1,3,2]{2,3,1,0:T(2,128)} %param.11) | data formatting | bytes 48 | tf_op args[3]
  2.0 0.7 %reshape.20.off_s = s32[6]{0:T(128)} reshape(s32[1,1,3,2]{3,2,1,0:T(4,128)S(1)} %copy.11) | data formatting | bytes 48 | tf_op jit(solution)/shard_map/reshape | solution.py:475
  2.7 1.3 %copy.14 = f32[1,1,3,16]{3,2,1,0:T(4,128)} copy(f32[1,1,3,16]{3,1,2,0:T(1,128)} %param.10) | data formatting | bytes 384
  4.0 0.7 %reduce = f32[3,16]{1,0:T(4,128)S(1)} reduce(f32[1,1,3,16]{3,1,2,0:T(1,128)} %param.10, f32[]{:T(128)} %constant.10), dimensions={0,1}, to_apply=%param.10.reduce_sub_computation | reduce | bytes 388 | tf_op args[2]
  4.7 0.6 reshape.19.w_s
  5.3 50.1 %shard_map.95 = (f32[2,128,128]{2,1,0:T(8,128)}, f32[2,16,128,128]{3,2,1,0:T(8,128)}) custom-call(f32[48]{0:T(128)} %reshape.19.w_s, s32[6]{0:T(128)} %reshape.20.off_s, s32[1]{0:T(128)} %bitcast.5.cnt_s, f32[2,128,128]{2,1,0:T(8,128)} %obj.1, bf16[2,16,128,128]{3,2,1,0:T(8,128)(2,1)} %eig.1, f32[3,16]{1,0:T(4,128)} %bitcast.7, ...), custom_call_target="tpu_custom_call" | custom-call | tf_op jit(solution)/shard_map/pallas_call | solution.py:443
  55.4 1.6 %copy.18 = f32[2,128,128]{2,1,0:T(8,128)} copy(f32[2,128,128]{2,1,0:T(8,128)} %get-tuple-element.4) | data formatting | bytes 262144
  56.9 3.1 %copy.19 = f32[2,16,128,128]{3,2,1,0:T(8,128)} copy(f32[2,16,128,128]{3,2,1,0:T(8,128)} %get-tuple-element.5) | data formatting | bytes 4194304

commit v2 on v1

--- a/solution.py
+++ b/solution.py
@@ -138,7 +138,7 @@
 
 
 def fused_kernel(
-    ntx, nty, w_s, off_s, cnt_s, obj, eig, w_v, amps, tab_r, tab_l, out_obj, out_eig,
+    ntx, nty, w_s, off_s, cnt_s, obj, eig, amps, tab_r, tab_l, out_obj, out_eig,
     below, right, diag, probe, win, acc, in_right, in_diag, in_below, msg, msg_all, grads, grads_all, upd,
     halo_ss, halo_rs, msg_ss, msg_rs, a2a_ss, a2a_rs, sp_ss, sp_rs, gat_ss, gat_rs,
 ):
@@ -168,15 +168,8 @@
     barrier = pltpu.get_barrier_semaphore()
     for a, b in peers:
         pl.semaphore_signal(barrier, inc=1, device_id=at(a, b), device_id_type=MESH)
-    pl.semaphore_wait(barrier, n - 1)
-
-    halo = []
-    for c in range(2):
-        halo.append(send(obj.at[c], below.at[c], halo_ss.at[c], halo_rs.at[c], at(-1, 0)))
-    for c in range(2):
-        halo.append(send(obj.at[c], right.at[c], halo_ss.at[2 + c], halo_rs.at[2 + c], at(0, -1)))
-
-    lives = [jnp.where(s < cnt_s[0], jnp.float32(1.0), jnp.float32(0.0)) for s in range(slots)]
+
+    lives = [jnp.where(s < cnt_s[0, 0], jnp.float32(1.0), jnp.float32(0.0)) for s in range(slots)]
     step = 32
 
     def probe_rows(i, total):
@@ -186,7 +179,7 @@
             for c in range(2):
                 e = eig[c, k, rows, :].astype(jnp.float32)
                 for s in range(slots):
-                    term = w_s[s * modes + k] * e
+                    term = w_s[0, 0, s, k] * e
                     parts[s][c] = term if k == 0 else parts[s][c] + term
         for s in range(slots):
             probe[s, 0, rows, :] = parts[s][0]
@@ -197,11 +190,22 @@
 
     total = lax.fori_loop(0, frame // step, probe_rows, jnp.zeros((1, frame), jnp.float32))
 
-    msg[...] = jnp.zeros_like(msg)
-    wv = w_v[...]
-    slot_id = lax.broadcasted_iota(jnp.int32, wv.shape, 0)
-    msg[0:slots, 0:modes] = wv
-    msg[slots : 2 * slots, 0:modes] = jnp.where(slot_id < cnt_s[0], wv * wv, 0.0)
+    pl.semaphore_wait(barrier, n - 1)
+    halo = []
+    for c in range(2):
+        halo.append(send(obj.at[c], below.at[c], halo_ss.at[c], halo_rs.at[c], at(-1, 0)))
+    for c in range(2):
+        halo.append(send(obj.at[c], right.at[c], halo_ss.at[2 + c], halo_rs.at[2 + c], at(0, -1)))
+
+    spot_row = lax.broadcasted_iota(jnp.int32, msg.shape, 0)
+    spot_lane = lax.broadcasted_iota(jnp.int32, msg.shape, 1)
+    table = jnp.zeros(msg.shape, jnp.float32)
+    for s in range(slots):
+        for k in range(modes):
+            w = w_s[0, 0, s, k]
+            column = jnp.where(spot_row == s, w, jnp.where(spot_row == slots + s, w * w * lives[s], 0.0))
+            table = jnp.where((spot_lane == k) & (spot_row % slots == s) & (spot_row < 2 * slots), column, table)
+    msg[...] = table
     msg[2 * slots : 2 * slots + 1, :] = total
     mine = pl.ds(pl.multiple_of(me * mrows, mrows), mrows)
     msg_all[mine, :] = msg[...]
@@ -211,7 +215,7 @@
 
     lane = lax.broadcasted_iota(jnp.int32, (frame, frame), 1)
     row = lax.broadcasted_iota(jnp.int32, (frame, frame), 0)
-    starts = [(off_s[2 * s], off_s[2 * s + 1]) for s in range(slots)]
+    starts = [(off_s[0, 0, s, 0], off_s[0, 0, s, 1]) for s in range(slots)]
 
     def spread(channel, piece_of):
         quads = [None] * 4
@@ -365,61 +369,106 @@
         flat_row = i * share
         return (flat_row // frame, pl.multiple_of(lax.rem(flat_row, frame), share))
 
-    def rows_of(a, b):
-        to = at(a, b)
-        z, start = place(to["tx"] * nty + to["ty"])
-        return out_eig.at[z, :, pl.ds(start, share), :]
-
     z, start = place(me)
     own = eig[z, :, pl.ds(start, share), :].astype(jnp.float32)
     out_eig[z, :, pl.ds(start, share), :] = own + upd[...].reshape(modes, share, frame)
 
     core = lax.rem(ty, 2)
-    ty_of = lambda j: lax.rem(ty + 2 * j, nty)
     other = {"tx": tx, "ty": ty + 1 - 2 * core}
-
-    def gathered(d, j):
-        z, start = place(lax.rem(tx - d + ntx, ntx) * nty + lax.rem(ty - 2 * j + nty, nty))
-        return out_eig.at[z, :, pl.ds(start, share), :]
-
-    def pass_on(d, j, kind, to):
-        ref = gathered(d, j)
-        k = (kind * ntx + d) * nx + j
-        return send(ref, ref, gat_ss.at[k], gat_rs.at[k], to)
-
-    along = {}
-    across = {}
-    over = []
-
-    def hop(ref, kind, d, j, to):
-        k = (kind * ntx + d) * nx + j
-        return send(ref, ref, gat_ss.at[k], gat_rs.at[k], to)
-
-    for d in range(1, ntx):
-        along[d] = hop(gathered(0, 0), 0, d, 0, at(d, 0))
+    part = modes // 2
+    used = []
+    always = tx >= 0
+
+    def inside(t):
+        return (t >= 0) & (t < ntx)
+
+    def hop(h, t, j, to, cond):
+        z, start = place(lax.rem(t + ntx, ntx) * nty + lax.rem(ty - 2 * j + nty, nty))
+        ref = out_eig.at[z, pl.ds(h * part, part), pl.ds(start, share), :]
+        k = len(used)
+        copy = pltpu.make_async_remote_copy(
+            src_ref=ref, dst_ref=ref, send_sem=gat_ss.at[k], recv_sem=gat_rs.at[k],
+            device_id=to, device_id_type=MESH,
+        )
+        used.append((copy, cond))
+        return copy
+
+    ways = [(w, e) for e in range(ntx - 1) for w in (1, -1)]
+    kinds = [(0, 0)] + [(1, j) for j in range(nx)]
+    got = {(w, e): inside(tx - w * (e + 1)) for w, e in ways}
+    chain = {
+        (w, e, h, j): hop(h, tx - w * e, j, at(w, 0), inside(tx - w * e) & inside(tx + w))
+        for w, e in ways
+        for h, j in kinds
+    }
+    across_own = {(h, j): hop(h, tx, 0, at(0, 2 * j), always) for h in (1, 0) for j in range(1, nx)}
+    across = {
+        (w, e, j): hop(0, tx - w * (e + 1), 0, at(0, 2 * j), got[w, e]) for w, e in ways for j in range(1, nx)
+    }
+    over_own = {(h, j): hop(h, tx, j, other, always) for h in (0, 1) for j in range(nx)}
+    over = {
+        (w, e, h, j): hop(h, tx - w * (e + 1), j, other, got[w, e])
+        for w, e in ways
+        for h in (0, 1)
+        for j in range(nx)
+    }
+
+    def start_chain(h, j):
+        for w in (1, -1):
+            pl.when(inside(tx + w))(chain[w, 0, h, j].start)
+
+    start_chain(1, 0)
+    start_chain(0, 0)
+    for h in (1, 0):
+        for j in range(1, nx):
+            across_own[h, j].start()
+    for h in (1, 0):
+        over_own[h, 0].start()
     for j in range(1, nx):
-        across[0, j] = hop(gathered(0, 0), 1, 0, j, at(0, 2 * j))
-    over.append(hop(gathered(0, 0), 2, 0, 0, other))
-    for d in range(1, ntx):
-        along[d].wait_recv()
-        for j in range(1, nx):
-            across[d, j] = hop(gathered(d, 0), 1, d, j, at(0, 2 * j))
-        over.append(hop(gathered(d, 0), 2, d, 0, other))
-
-    for k in range(3, 9):
-        spill[k].wait_recv()
-    illum = acc[0, 2] + in_right[2] + in_below[2] + mean
-    for c in range(2):
-        out_obj[c] = obj[c] + (acc[0, c] + in_right[c] + in_below[c]) / illum
-
-    for d in range(ntx):
-        for j in range(1, nx):
-            across[d, j].wait_recv()
-            over.append(hop(gathered(d, j), 2, d, j, other))
-    for copy in over:
+        across_own[1, j].wait_recv()
+        start_chain(1, j)
+        over_own[1, j].start()
+
+    def arrive(w, e, h, j):
+        chain[w, e, h, j].wait_recv()
+        if e + 1 < ntx - 1:
+            pl.when(inside(tx + w))(chain[w, e + 1, h, j].start)
+        if h == 0:
+            for k in range(1, nx):
+                across[w, e, k].start()
+        over[w, e, h, j].start()
+
+    for e in range(ntx - 1):
+        for h, j in [(1, 0), (0, 0)] + [(1, j) for j in range(1, nx)]:
+            for w in (1, -1):
+                pl.when(got[w, e])(functools.partial(arrive, w, e, h, j))
+        if e == 0:
+            for k in range(3, 9):
+                spill[k].wait_recv()
+            illum = acc[0, 2] + in_right[2] + in_below[2] + mean
+            for c in range(2):
+                out_obj[c] = obj[c] + (acc[0, c] + in_right[c] + in_below[c]) / illum
+
+    def cross(w, e, j):
+        across[w, e, j].wait_recv()
+        over[w, e, 0, j].start()
+
+    for j in range(1, nx):
+        across_own[0, j].wait_recv()
+        over_own[0, j].start()
+        for w, e in ways:
+            pl.when(got[w, e])(functools.partial(cross, w, e, j))
+    for copy in over_own.values():
         copy.wait_recv()
-    for copy in halo + msgs + swaps + spill + list(along.values()) + list(across.values()) + over:
+    for (w, e, h, j), copy in over.items():
+        pl.when(got[w, e])(copy.wait_recv)
+    for copy in halo + msgs + swaps + spill:
         copy.wait_send()
+    for copy, cond in used:
+        if cond is always:
+            copy.wait_send()
+        else:
+            pl.when(cond)(copy.wait_send)
 
 
 def per_device_fused(mesh, obj_field, eigenprobes, weights, offsets, counts, amplitudes):
@@ -428,7 +477,9 @@
     tile, width = obj_field.shape[1:]
     _, modes, frame, _ = eigenprobes.shape
     slots = weights.shape[2]
-    fits = tile == width == frame and frame % 128 == 0 and nty % 2 == 0 and n % 8 == 0
+    hops = 2 * (ntx - 1)
+    copies = hops * (1 + nty // 2) + (nty // 2 - 1) * (2 + hops) + nty * (1 + hops)
+    fits = tile == width == frame and frame % 128 == 0 and nty % 2 == 0 and n % 8 == 0 and modes % 2 == 0
     if not (fits and (2 * frame) % (16 * n) == 0 and frame % (2 * frame // n) == 0):
         return per_device(obj_field, eigenprobes, weights, offsets, counts, amplitudes)
     share = 2 * frame // n
@@ -436,17 +487,16 @@
     tab_r, tab_l = dft_tables(frame)
     vmem = pl.BlockSpec(memory_space=pltpu.VMEM)
     smem = pl.BlockSpec(memory_space=pltpu.SMEM)
-    nx = nty // 2
     f32 = jnp.float32
     square = (frame, frame)
     dma = pltpu.SemaphoreType.DMA
     return tuple(pl.pallas_call(
         functools.partial(fused_kernel, ntx, nty),
         out_shape=(
-            jax.ShapeDtypeStruct(obj_field.shape, f32),
-            jax.ShapeDtypeStruct(eigenprobes.shape, f32),
+            pltpu.VMEM(obj_field.shape, f32),
+            pltpu.VMEM(eigenprobes.shape, f32),
         ),
-        in_specs=[smem] * 3 + [vmem] * 6,
+        in_specs=[smem] * 3 + [vmem] * 5,
         out_specs=(vmem, vmem),
         scratch_shapes=[
             pltpu.VMEM((2,) + square, f32),
@@ -467,16 +517,15 @@
             dma((n - 1,)), dma((n - 1,)),
             dma((n - 1,)), dma((n - 1,)),
             dma((9,)), dma((9,)),
-            dma((3 * ntx * nx,)), dma((3 * ntx * nx,)),
+            dma((copies,)), dma((copies,)),
         ],
         compiler_params=pltpu.CompilerParams(collective_id=0, has_side_effects=True),
     )(
-        weights.reshape(slots * modes),
-        offsets.reshape(slots * 2),
-        counts.reshape(1),
+        weights,
+        offsets,
+        counts,
         obj_field,
         eigenprobes,
-        weights.reshape(slots, modes),
         amplitudes.reshape((slots,) + square),
         jnp.asarray(tab_r),
         jnp.asarray(tab_l),

time: 60.9 us -> 54 us (0.89); the launches traced: 60.1 us -> 53.8 us
  local copies, waits for them, and re-layouts: 7.98 us -> 4.57 us
  Pallas kernels: 50.1 us -> 48 us
  other arithmetic: 0.7 us -> 0 us
    unnamed x4, local copies, waits for them, and re-layouts: 6.73 us -> 4.57 us
    pallas_call x1, Pallas kernels: 50.1 us -> 48 us  [per_device_fused(): pl.pallas_call(functools.partial(fused_kernel, ntx, nty), out_shape=(pltp...]
    reshape x2 -> x0, local copies, waits for them, and re-layouts: 1.26 us -> none  [the longest x1 0.66 us: per_device_fused(): offsets.reshape(slots * 2)]
    unnamed x1 -> x0, other arithmetic: 0.7 us -> none
where the time goes in v2:
time: 54 us; the launch traced here: 53.8 us
  Pallas kernels  48 us (89%)
  local copies, waits for them, and re-layouts  4.57 us (8%)
  between operations  1.29 us (2%)
    pallas_call x1, Pallas kernels, per_device_fused(): pl.pallas_call(functools.partial(fused_kernel, ntx, nty), out_shape=(pltp...  48 us
    unnamed x4, local copies, waits for them, and re-layouts  4.57 us

profile of v2, /device:TPU:0, one launch (start us, length us, event | category | flops | bytes accessed | tf_op | source)
XLA Modules:
  0.0 53.8 jit_solution(11230247156251639940)
XLA Ops:
  1.3 1.3 %copy.10.w_s = f32[1,1,3,16]{3,2,1,0:T(4,128)} copy(f32[1,1,3,16]{3,1,2,0:T(1,128)} %param.10) | data formatting | bytes 384 | tf_op args[2]
  2.5 1.3 %copy.11.off_s = s32[1,1,3,2]{3,2,1,0:T(4,128)} copy(s32[1,1,3,2]{2,3,1,0:T(2,128)} %param.11) | data formatting | bytes 48 | tf_op args[3]
  3.9 48.0 %shard_map.95 = (f32[2,128,128]{2,1,0:T(8,128)S(1)}, f32[2,16,128,128]{3,2,1,0:T(8,128)S(1)}) custom-call(f32[1,1,3,16]{3,2,1,0:T(4,128)} %copy.10.w_s, s32[1,1,3,2]{3,2,1,0:T(4,128)} %copy.11.off_s, s32[1,1]{1,0:T(1,128)S(6)} %copy.16.cnt_s, f32[2,128,128]{2,1,0:T(8,128)} %obj.1, bf16[2,16,128,128]{3,2,1,0:T(8,128)(2,1)} %eig.1, ...), custom_call_target="tpu_custom_call" | custom-call | tf_op jit(solution)/shard_map/pallas_call | solution.py:493
  51.8 0.7 %copy.14 = f32[2,128,128]{2,1,0:T(8,128)} copy(f32[2,128,128]{2,1,0:T(8,128)S(1)} %get-tuple-element.2) | data formatting | bytes 262144
  52.5 1.3 %copy.15 = f32[2,16,128,128]{3,2,1,0:T(8,128)} copy(f32[2,16,128,128]{3,2,1,0:T(8,128)S(1)} %get-tuple-element.3) | data formatting | bytes 4194304
